TPU v7x, 32 devices: a whole 2x2x4 slice. The times are simulated.
32 devices in a mesh: blk: 4 (over z), tp: 8 (over y, x, core).
Axes of the slice: x: 2, y: 2, z: 4, core: 2. Of those that a mesh axis runs over, the one named last changes fastest.
Arguments:
- input_pool: bfloat16 [4096, 1792], P(None, 'tp'), may hold values from -6 to 6
- teacher_pool: bfloat16 [4096, 1792], P(None, 'tp'), may hold values from -6 to 6
- gate_weight: bfloat16 [1792, 9472], P(None, 'tp'), may hold values from -0.125 to 0.125
- up_weight: bfloat16 [1792, 9472], P(None, 'tp'), may hold values from -0.125 to 0.125
- params: float32 [4, 9472, 1792], P('blk', 'tp'), may hold values from -6 to 6
- batch_ids: int32 [4, 1024], replicated, may hold values from 0 to 4095
- cycle_order: int32 [4], replicated, may hold values from 0 to 3, each once
- edge_weight: float32 [4], replicated, may hold values from 0.1 to 0.45
Outputs:
- updated: float32 [4, 9472, 1792], P('blk', 'tp')
Inputs may be any that keep to these rules, and one draw needn't show every extreme that they name: `cycle_order`: the 4 cycle positions name 4 different agents.
All inputs are finite; a program needn't handle non-finite values.
Results may differ from a plain program's by a relative error of at most 0.0061.
Values may be sent and summed in bfloat16 or wider, within the bound.
A program may use at most 128 MiB of HBM per device.

v0:
```python
import jax
import jax.numpy as jnp
from jax import lax
from jax.sharding import PartitionSpec as P


def shifted(array, axis, by):
    count = lax.axis_size(axis)
    return lax.ppermute(array, axis, [(i, (i + by) % count) for i in range(count)])


def body(
    input_pool, teacher_pool, gate_weight, up_weight, params, batch_ids, cycle_order, edge_weight
):
    step_rate = 2.0
    groups = lax.axis_size("tp")
    place = lax.axis_index("blk")
    agents = cycle_order.shape[0]
    slots = jnp.arange(agents, dtype=jnp.int32)
    here = slots == place
    before = slots == (place + agents - 1) % agents
    agent = jnp.sum(jnp.where(here, cycle_order, 0))
    weight_next = jnp.sum(jnp.where(here, edge_weight, 0.0))
    weight_prev = jnp.sum(jnp.where(before, edge_weight, 0.0))
    weight_self = 1.0 - weight_next - weight_prev
    batch = lax.dynamic_slice_in_dim(batch_ids, agent, 1, 0)[0]
    inputs_local = jnp.take(input_pool, batch, axis=0)
    teacher_local = jnp.take(teacher_pool, batch, axis=0)
    hidden_dev = gate_weight.shape[1]
    scale = float(hidden_dev * groups) ** (-0.5)
    rows = lax.all_gather(inputs_local, "tp", axis=1, tiled=True)
    gate = jnp.dot(rows, gate_weight, preferred_element_type=jnp.float32)
    up = jnp.dot(rows, up_weight, preferred_element_type=jnp.float32)
    teacher = lax.all_gather(teacher_local, "tp", axis=1, tiled=True)
    gate, up, teacher_full = (gate, up, teacher)
    hidden = (jax.nn.silu(gate) * up).astype(jnp.bfloat16)

    def gradient(weights):
        weights_half = weights.astype(jnp.bfloat16)
        partial_out = scale * jnp.dot(hidden, weights_half, preferred_element_type=jnp.float32)
        output = lax.psum(partial_out, "tp")
        resid = (output - teacher_full.astype(jnp.float32)).astype(jnp.bfloat16)
        return scale * lax.dot_general(
            hidden, resid, (((0,), (0,)), ((), ())), preferred_element_type=jnp.float32
        )

    start_field = params[0]
    grad_first = gradient(start_field)

    def mix_two(field):
        lower = shifted(field, "blk", 1)
        upper = shifted(field, "blk", -1)
        return weight_self * field + weight_next * upper + weight_prev * lower

    moved = mix_two(start_field) - step_rate * grad_first
    combined = moved - step_rate * grad_first
    grad_second = gradient(moved)
    result = mix_two(combined) - step_rate * (grad_second - grad_first)
    return result[None]


def solution(mesh):
    placed = (
        P(None, "tp"),
        P(None, "tp"),
        P(None, "tp"),
        P(None, "tp"),
        P("blk", "tp", None),
        P(),
        P(),
        P(),
    )
    return jax.shard_map(
        body, mesh=mesh, in_specs=placed, out_specs=P("blk", "tp", None), check_vma=False
    )
```

profile of v0, /device:TPU:0, one launch (start us, length us, event | category | flops | bytes accessed | tf_op | source)
XLA Modules:
  0.0 809.0 jit_solution(17603481513020024617)
XLA Ops:
  6.5 1.3 fusion.11
  9.8 4.0 copy.11
  13.8 3.2 copy.13
  17.0 5.3 gather_fusion
  22.4 3.9 gather_fusion.1
  26.5 1.0 copy.12
  28.6 5.1 collective-permute-start
  33.7 31.0 %all-gather.3.cloned.1.call-done = bf16[1024,1792]{0,1:T(8,128)(2,1)} async-done(((bf16[1024,224]{0,1:T(8,128)(2,1)}), bf16[1024,1792]{0,1:T(8,128)(2,1)}) %all-gather.3.cloned.1.call-update) | async-done | bytes 3670032 | tf_op jit(solution)/shard_map/all_gather | solution.py:31
  64.8 7.6 fusion.17
  72.4 8.0 multiply_convert_fusion
  80.4 1.5 copy-done.2
  81.8 7.2 convolution_multiply_fusion.2
  91.6 9.5 %all-gather.5.cloned.1.call-done = bf16[1024,1792]{0,1:T(8,128)(2,1)} async-done(((bf16[1024,224]{0,1:T(8,128)(2,1)}), bf16[1024,1792]{0,1:T(8,128)(2,1)}) %all-gather.5.cloned.1.call-update) | async-done | bytes 3670032 | tf_op jit(solution)/shard_map/all_gather | solution.py:34
  101.1 115.9 %collective-permute-done = f32[1184,1792]{1,0:T(8,128)} collective-permute-done((f32[1184,1792]{1,0:T(8,128)}, f32[1184,1792]{1,0:T(8,128)}, u32[]{:S(2)}, u32[]{:S(2)}) %collective-permute-start) | collective-permute-done | bytes 8486944 | tf_op jit(solution)/shard_map/ppermute | solution.py:9
  217.0 181.6 %collective-permute-done.1 = f32[1184,1792]{1,0:T(8,128)} collective-permute-done((f32[1184,1792]{1,0:T(8,128)}, f32[1184,1792]{1,0:T(8,128)}, u32[]{:S(2)}, u32[]{:S(2)}) %collective-permute-start.1) | collective-permute-done | bytes 8486944 | tf_op jit(solution)/shard_map/ppermute | solution.py:9
  398.6 22.6 %multiply_subtract_fusion = (f32[1184,1792]{1,0:T(8,128)}, bf16[1184,1792]{1,0:T(8,128)(2,1)S(1)}, f32[1184,1792]{1,0:T(8,128)}) fusion(f32[1184,1792]{1,0:T(8,128)} %collective-permute-done.1, f32[]{:T(128)} %get-tuple-element.7, f32[1184,1792]{1,0:T(8,128)} %collective-permute-done, f32[]{:T(128)} %get-tuple-element.6, f32[1,1184,1792]{2,1,0:T(8,128)} %param.14, ...), kind=kOutput, calls=%fused_computation.9 | convolution fusion | flops 4369899520 | bytes 60112908 | tf_op jit(solution)/shard_map/dot_general | solution.py:43
  421.2 1.6 collective-permute-start.3
  422.9 2.2 collective-permute-start.2
  425.1 8.7 %convolution_multiply_fusion.1 = f32[1024,1792]{0,1:T(8,128)} fusion(bf16[1024,1184]{0,1:T(8,128)(2,1)} %copy-done.2, bf16[1184,1792]{1,0:T(8,128)(2,1)S(1)} %get-tuple-element.9), kind=kOutput, calls=%fused_computation.13 | convolution fusion | flops 4347133952 | bytes 14008320 | tf_op jit(solution)/shard_map/dot_general | solution.py:40
  433.8 113.8 %all-reduce.5.cloned.1.call-done = f32[1024,1792]{0,1:T(8,128)} async-done(((f32[1024,1792]{0,1:T(8,128)}), f32[1024,1792]{0,1:T(8,128)}) %all-reduce.5.cloned.1.call-update) | async-done | bytes 7340048 | tf_op jit(solution)/shard_map/psum | solution.py:41
  547.6 12.8 %fusion.1 = f32[1184,1792]{1,0:T(8,128)} fusion(bf16[1024,1184]{0,1:T(8,128)(2,1)S(1)} %copy-done.3, f32[1184,1792]{1,0:T(8,128)} %get-tuple-element.12, f32[1024,1792]{0,1:T(8,128)} %all-reduce.5.cloned.1.call-done, bf16[1024,1792]{0,1:T(8,128)(2,1)} %all-gather.5.cloned.1.call-done), kind=kOutput, calls=%fused_computation.6 | convolution fusion | flops 4359290880 | bytes 30408704 | tf_op jit(solution)/shard_map/dot_general | solution.py:43
  560.5 48.3 %collective-permute-done.3 = f32[1184,1792]{1,0:T(8,128)} collective-permute-done((f32[1184,1792]{1,0:T(8,128)}, f32[1184,1792]{1,0:T(8,128)}, u32[]{:S(2)}, u32[]{:S(2)}) %collective-permute-start.3) | collective-permute-done | bytes 8486944 | tf_op jit(solution)/shard_map/ppermute | solution.py:9
  608.8 179.5 %collective-permute-done.2 = f32[1184,1792]{1,0:T(8,128)} collective-permute-done((f32[1184,1792]{1,0:T(8,128)}, f32[1184,1792]{1,0:T(8,128)}, u32[]{:S(2)}, u32[]{:S(2)}) %collective-permute-start.2) | collective-permute-done | bytes 8486944 | tf_op jit(solution)/shard_map/ppermute | solution.py:9
  788.3 14.1 %subtract_bitcast_fusion = f32[1,1184,1792]{2,1,0:T(8,128)} fusion(f32[1184,1792]{1,0:T(8,128)} %fusion.1, f32[1184,1792]{1,0:T(8,128)} %collective-permute-done.3, f32[1184,1792]{1,0:T(8,128)} %collective-permute-done.2, f32[1184,1792]{1,0:T(8,128)S(1)} %bitcast.29, f32[]{:T(128)} %get-tuple-element.7, f32[]{:T(128)} %get-tuple-element.6, f32[]{:T(128)S(6)} %sub.29), kind=kLoop, calls=%fused_computation.7 | loop fusion | flops 12730368 | bytes 42434572 | tf_op jit(solution)/shard_map/broadcast_in_dim | solution.py:59
  (41 shorter events, 2.7 us)
Async XLA Ops:
  6.5 3.3 copy-start
  6.5 58.2 %all-gather.3.cloned.1.call-start = ((), (), s32[]{:S(2)}) async-start(), calls=%async_computation | async-start | bytes 4128768 | tf_op jit(solution)/shard_map/all_gather | solution.py:31
  27.5 73.6 %all-gather.5.cloned.1.call-start = ((), (), s32[]{:S(2)}) async-start(), calls=%async_computation.2 | async-start | bytes 4128768 | tf_op jit(solution)/shard_map/all_gather | solution.py:34
  28.5 370.1 %all-reduce.3.cloned.1.call-start = ((), (), s32[]{:S(2)}) async-start(), calls=%async_computation.1 | async-start | bytes 14680064 | tf_op jit(solution)/shard_map/psum | solution.py:41
  28.6 188.4 %collective-permute-start = (f32[1184,1792]{1,0:T(8,128)}, f32[1184,1792]{1,0:T(8,128)}, u32[]{:S(2)}, u32[]{:S(2)}) collective-permute-start(f32[1184,1792]{1,0:T(8,128)} %bitcast.30), channel_id=1, source_target_pairs={{0,24},{8,0},{16,8},{24,16},{1,25},{9,1},{17,9},{25,17},{2,26},{10... | collective-permute-start | bytes 25460744 | tf_op jit(solution)/shard_map/ppermute | solution.py:9
  33.7 364.9 %collective-permute-start.1 = (f32[1184,1792]{1,0:T(8,128)}, f32[1184,1792]{1,0:T(8,128)}, u32[]{:S(2)}, u32[]{:S(2)}) collective-permute-start(f32[1184,1792]{1,0:T(8,128)} %bitcast.31), channel_id=1, source_target_pairs={{0,8},{8,16},{16,24},{24,0},{1,9},{9,17},{17,25},{25,1},{2,10},{10... | collective-permute-start | bytes 25460744 | tf_op jit(solution)/shard_map/ppermute | solution.py:9
  64.8 7.6 copy-start.5
  64.8 17.1 %slice-start.3 = ((s8[8486912]{0:T(1024)(128)(4,1)}), s8[4194304]{0:T(1024)(128)(4,1)S(1)}, s32[]{:S(2)}) async-start(s8[8486912]{0:T(1024)(128)(4,1)} %bitcast.32), calls=%async_computation.7 | async-start | bytes 8388608
  64.8 17.1 %slice-start.4 = ((s8[8486912]{0:T(1024)(128)(4,1)}), s8[4194304]{0:T(1024)(128)(4,1)S(1)}, s32[]{:S(2)}) async-start(s8[8486912]{0:T(1024)(128)(4,1)} %bitcast.32), calls=%async_computation.8 | async-start | bytes 8388608
  72.4 9.5 %slice-start.5 = ((s8[8486912]{0:T(1024)(128)(4,1)}), s8[98304]{0:T(1024)(128)(4,1)S(1)}, s32[]{:S(2)}) async-start(s8[8486912]{0:T(1024)(128)(4,1)} %bitcast.32), calls=%async_computation.9 | async-start | bytes 196608
  80.4 1.5 copy-start.2
  89.1 0.7 copy-start.4
  89.1 458.6 %all-reduce.5.cloned.1.call-start = ((), (), s32[]{:S(2)}) async-start(), calls=%async_computation.3 | async-start | bytes 14680064 | tf_op jit(solution)/shard_map/psum | solution.py:41
  421.2 187.5 %collective-permute-start.3 = (f32[1184,1792]{1,0:T(8,128)}, f32[1184,1792]{1,0:T(8,128)}, u32[]{:S(2)}, u32[]{:S(2)}) collective-permute-start(f32[1184,1792]{1,0:T(8,128)} %get-tuple-element.8), channel_id=1, source_target_pairs={{0,8},{8,16},{16,24},{24,0},{1,9},{9,17},{17,25},{25,1},{2,10},{10... | collective-permute-start | bytes 25460744 | tf_op jit(solution)/shard_map/ppermute | solution.py:9
  422.9 365.4 %collective-permute-start.2 = (f32[1184,1792]{1,0:T(8,128)}, f32[1184,1792]{1,0:T(8,128)}, u32[]{:S(2)}, u32[]{:S(2)}) collective-permute-start(f32[1184,1792]{1,0:T(8,128)} %get-tuple-element.8), channel_id=1, source_target_pairs={{0,24},{8,0},{16,8},{24,16},{1,25},{9,1},{17,9},{25,17},{2,26},{10... | collective-permute-start | bytes 25460744 | tf_op jit(solution)/shard_map/ppermute | solution.py:9
  433.8 113.8 %copy-start.3 = (bf16[1024,1184]{0,1:T(8,128)(2,1)S(1)}, bf16[1024,1184]{0,1:T(8,128)(2,1)}, u32[]{:S(2)}) copy-start(bf16[1024,1184]{0,1:T(8,128)(2,1)} %copy-done.2) | copy-start | bytes 7274500
  433.8 354.5 %slice-start = ((s8[8486912]{0:T(1024)(128)(4,1)}), s8[98304]{0:T(1024)(128)(4,1)S(1)}, s32[]{:S(2)}) async-start(s8[8486912]{0:T(1024)(128)(4,1)} %bitcast.28), calls=%async_computation.4 | async-start | bytes 196608
  547.6 240.6 %slice-start.1 = ((s8[8486912]{0:T(1024)(128)(4,1)}), s8[4194304]{0:T(1024)(128)(4,1)S(1)}, s32[]{:S(2)}) async-start(s8[8486912]{0:T(1024)(128)(4,1)} %bitcast.28), calls=%async_computation.5 | async-start | bytes 8388608
  547.6 240.6 %slice-start.2 = ((s8[8486912]{0:T(1024)(128)(4,1)}), s8[4194304]{0:T(1024)(128)(4,1)S(1)}, s32[]{:S(2)}) async-start(s8[8486912]{0:T(1024)(128)(4,1)} %bitcast.28), calls=%async_computation.6 | async-start | bytes 8388608
  788.3 14.2 %copy-start.1 = (s32[4,1024]{1,0:T(4,128)S(1)}, s32[4,1024]{1,0:T(4,128)}, u32[]{:S(2)}) copy-start(s32[4,1024]{1,0:T(4,128)} %param.15) | copy-start | bytes 49156
Sparse Core Ops, SparseCore 0:
  27.6 37.0 all-gather.2
  66.7 34.3 all-gather.4
  104.4 115.4 all-reduce.2
  433.9 113.6 all-reduce.4
where the time goes:
time: 809 us
  waiting for transfers between devices  680 us (84%)
  matrix products  66.9 us (8%)
  local copies, waits for them, and re-layouts  20.5 us (3%)
  between operations  16.4 us (2%)
  other arithmetic  16.3 us (2%)
  starting transfers between devices  9.08 us (1%)
    ppermute x4, waiting for transfers between devices, shifted(): lax.ppermute(array, axis, [(i, (i + by) % count) for i in range(count)])  525 us
    psum x2, waiting for transfers between devices, gradient(): output = lax.psum(partial_out, 'tp')  114 us
    dot_general x2, matrix products, gradient(): lax.dot_general(hidden, resid, (((0,), (0,)), ((), ())), preferred_elemen...  35.4 us
    all_gather x1, waiting for transfers between devices, body(): rows = lax.all_gather(inputs_local, 'tp', axis=1, tiled=True)  31 us
  transfers between devices with their start and end apart: 8, of which 7 were waited for; matrix products, arithmetic and copies ran while one was open for 6% of the time, Pallas kernels for 0%

commit v1 on v0

--- a/solution.py
+++ b/solution.py
@@ -1,7 +1,28 @@
+import functools
 import jax
 import jax.numpy as jnp
 from jax import lax
 from jax.sharding import PartitionSpec as P
+
+
+def name_target_in(content, chip_axis):
+    amount_of = jax.lax.axis_size(chip_axis)
+
+    def sample_replace(tmp, last):
+        if last >= amount_of:
+            return tmp
+        return sample_replace(
+            tmp
+            + jax.lax.ppermute(
+                tmp, chip_axis, list(map(lambda h: (h, h ^ last), range(amount_of)))
+            ),
+            2 * last,
+        )
+
+    return sample_replace(content, 1)
+
+
+wrap_orders_up = functools.partial(name_target_in, chip_axis="tp")
 
 
 def shifted(array, axis, by):
@@ -38,7 +59,7 @@
     def gradient(weights):
         weights_half = weights.astype(jnp.bfloat16)
         partial_out = scale * jnp.dot(hidden, weights_half, preferred_element_type=jnp.float32)
-        output = lax.psum(partial_out, "tp")
+        output = wrap_orders_up(partial_out)
         resid = (output - teacher_full.astype(jnp.float32)).astype(jnp.bfloat16)
         return scale * lax.dot_general(
             hidden, resid, (((0,), (0,)), ((), ())), preferred_element_type=jnp.float32

time: 809 us -> 930 us (1.15)
  waiting for transfers between devices: 680 us -> 756 us
  local copies, waits for them, and re-layouts: 20.5 us -> 36.9 us
  matrix products: 66.9 us -> 79.6 us
  other arithmetic: 16.3 us -> 28.3 us
    ppermute x0 -> x6, waiting for transfers between devices: none -> 328 us  [sample_replace(): jax.lax.ppermute(tmp, chip_axis, list(map(lambda h: (h, h ^ last), range(...]
    ppermute x4, waiting for transfers between devices: 525 us -> 343 us  [shifted(): lax.ppermute(array, axis, [(i, (i + by) % count) for i in range(count)])]
    psum x2 -> x0, waiting for transfers between devices: 114 us -> none  [gradient(): output = lax.psum(partial_out, 'tp')]
    all_gather x1, waiting for transfers between devices: 9.5 us -> 47.7 us  [body(): teacher = lax.all_gather(teacher_local, 'tp', axis=1, tiled=True)]
    add x0 -> x4, other arithmetic: none -> 25 us  [sample_replace(): tmp + jax.lax.ppermute(tmp, chip_axis, list(map(lambda h: (h, h ^ last),...]
    dot_general x2, matrix products: 35.4 us -> 50.6 us  [gradient(): lax.dot_general(hidden, resid, (((0,), (0,)), ((), ())), preferred_elemen...]
    broadcast_in_dim x1 -> x0, other arithmetic: 14.1 us -> none  [body(): return result[None]]
    unnamed x26, local copies, waits for them, and re-layouts: 9.26 us -> 18.7 us
  transfers between devices with their start and end apart: 8 -> 12, of which waited for: 7 -> 9; matrix products, arithmetic and copies ran while one was open for 6% -> 2% of each run, Pallas kernels for 0% -> 0%
where the time goes in v1:
time: 930 us
  waiting for transfers between devices  756 us (81%)
  matrix products  79.6 us (9%)
  local copies, waits for them, and re-layouts  36.9 us (4%)
  other arithmetic  28.3 us (3%)
  between operations  16.8 us (2%)
  starting transfers between devices  12.1 us (1%)
    ppermute x4, waiting for transfers between devices, shifted(): lax.ppermute(array, axis, [(i, (i + by) % count) for i in range(count)])  343 us
    ppermute x6, waiting for transfers between devices, sample_replace(): jax.lax.ppermute(tmp, chip_axis, list(map(lambda h: (h, h ^ last), range(...  328 us
    dot_general x2, matrix products, gradient(): lax.dot_general(hidden, resid, (((0,), (0,)), ((), ())), preferred_elemen...  50.6 us
    all_gather x1, waiting for transfers between devices, body(): teacher = lax.all_gather(teacher_local, 'tp', axis=1, tiled=True)  47.7 us
    all_gather x1, waiting for transfers between devices, body(): rows = lax.all_gather(inputs_local, 'tp', axis=1, tiled=True)  37.2 us
    add x4, other arithmetic, sample_replace(): tmp + jax.lax.ppermute(tmp, chip_axis, list(map(lambda h: (h, h ^ last),...  25 us
    unnamed x26, local copies, waits for them, and re-layouts  18.7 us
  transfers between devices with their start and end apart: 12, of which 9 were waited for; matrix products, arithmetic and copies ran while one was open for 2% of the time, Pallas kernels for 0%

profile of v1, /device:TPU:0, one launch (start us, length us, event | category | flops | bytes accessed | tf_op | source)
XLA Modules:
  0.0 929.8 jit_solution(13921809371300892428)
XLA Ops:
  9.8 4.0 copy.13
  13.8 3.2 copy.11
  17.0 5.3 gather_fusion.1
  22.4 5.0 gather_fusion
  29.6 37.2 %all-gather.3.cloned.1.call-done = bf16[1024,1792]{0,1:T(8,128)(2,1)} async-done(((bf16[1024,224]{0,1:T(8,128)(2,1)}), bf16[1024,1792]{0,1:T(8,128)(2,1)}) %all-gather.3.cloned.1.call-update) | async-done | bytes 3670032 | tf_op jit(solution)/shard_map/all_gather | solution.py:52
  66.9 7.6 fusion.17
  74.4 7.7 multiply_convert_fusion
  82.2 5.2 convolution_multiply_fusion.2
  90.5 8.8 collective-permute-done.2
  99.3 6.1 add.56
  110.7 154.9 %collective-permute-done.3 = f32[1024,1792]{1,0:T(8,128)} collective-permute-done((f32[1024,1792]{1,0:T(8,128)S(1)}, f32[1024,1792]{1,0:T(8,128)}, u32[]{:S(2)}, u32[]{:S(2)}) %collective-permute-start.3) | collective-permute-done | bytes 7340064 | tf_op jit(solution)/shard_map/ppermute | solution.py:16
  265.7 6.8 add.57
  276.8 47.7 %all-gather.5.cloned.1.call-done = bf16[1024,1792]{0,1:T(8,128)(2,1)} async-done(((bf16[1024,224]{0,1:T(8,128)(2,1)}), bf16[1024,1792]{0,1:T(8,128)(2,1)}) %all-gather.5.cloned.1.call-update) | async-done | bytes 3670032 | tf_op jit(solution)/shard_map/all_gather | solution.py:55
  324.5 6.0 copy.15
  330.5 144.3 %collective-permute-done = f32[1184,1792]{1,0:T(8,128)} collective-permute-done((f32[1184,1792]{1,0:T(8,128)}, f32[1184,1792]{1,0:T(8,128)}, u32[]{:S(2)}, u32[]{:S(2)}) %collective-permute-start) | collective-permute-done | bytes 8486944 | tf_op jit(solution)/shard_map/ppermute | solution.py:30
  474.7 26.8 %multiply_subtract_fusion = (f32[1184,1792]{1,0:T(8,128)}, f32[1184,1792]{1,0:T(8,128)}, f32[1184,1792]{1,0:T(8,128)}) fusion(f32[1184,1792]{1,0:T(8,128)} %collective-permute-done.1, f32[]{:T(128)} %get-tuple-element.7, f32[1184,1792]{1,0:T(8,128)} %collective-permute-done, f32[]{:T(128)} %get-tuple-element.6, f32[1,1184,1792]{2,1,0:T(8,128)} %param.14, ...), kind=kOutput, calls=%fused_computation.9 | convolution fusion | flops 4369612800 | bytes 71696400 | tf_op jit(solution)/shard_map/dot_general | solution.py:64
  501.6 8.6 convolution_multiply_fusion.1
  513.1 9.0 collective-permute-done.7
  522.0 6.1 add.61
  532.6 155.7 %collective-permute-done.8 = f32[1024,1792]{1,0:T(8,128)} collective-permute-done((f32[1024,1792]{1,0:T(8,128)S(1)}, f32[1024,1792]{1,0:T(8,128)}, u32[]{:S(2)}, u32[]{:S(2)}) %collective-permute-start.8) | collective-permute-done | bytes 7340064 | tf_op jit(solution)/shard_map/ppermute | solution.py:16
  688.3 6.1 add.62
  697.8 18.5 %collective-permute-done.6 = f32[1184,1792]{1,0:T(8,128)} collective-permute-done((f32[1184,1792]{1,0:T(8,128)}, f32[1184,1792]{1,0:T(8,128)}, u32[]{:S(2)}, u32[]{:S(2)}) %collective-permute-start.6) | collective-permute-done | bytes 8486944 | tf_op jit(solution)/shard_map/ppermute | solution.py:30
  716.3 179.8 %collective-permute-done.5 = f32[1184,1792]{1,0:T(8,128)} collective-permute-done((f32[1184,1792]{1,0:T(8,128)}, f32[1184,1792]{1,0:T(8,128)}, u32[]{:S(2)}, u32[]{:S(2)}) %collective-permute-start.5) | collective-permute-done | bytes 8486944 | tf_op jit(solution)/shard_map/ppermute | solution.py:30
  899.2 23.7 %subtract_bitcast_fusion = f32[1,1184,1792]{2,1,0:T(8,128)} fusion(f32[1184,1792]{1,0:T(8,128)} %collective-permute-done.6, f32[1184,1792]{1,0:T(8,128)} %collective-permute-done.5, f32[1184,1792]{1,0:T(8,128)} %get-tuple-element.12, bf16[1024,1184]{0,1:T(8,128)(2,1)S(1)} %multiply_convert_fusion, f32[]{:T(128)} %get-tuple-element.7, f32[]{:T(128)} %get-tuple-element.6, ...), kind=kOutput, calls=%fused_computation.7 | convolution fusion | flops 4378099712 | bytes 63209484 | tf_op jit(solution)/shard_map/dot_general | solution.py:64
  (50 shorter events, 28.8 us)
Async XLA Ops:
  6.5 3.3 copy-start
  6.5 60.3 %all-gather.3.cloned.1.call-start = ((), (), s32[]{:S(2)}) async-start(), calls=%async_computation | async-start | bytes 4128768 | tf_op jit(solution)/shard_map/all_gather | solution.py:52
  29.6 294.9 %all-gather.5.cloned.1.call-start = ((), (), s32[]{:S(2)}) async-start(), calls=%async_computation.1 | async-start | bytes 4128768 | tf_op jit(solution)/shard_map/all_gather | solution.py:55
  66.8 7.6 copy-start.8
  66.9 15.3 %slice-start = ((s8[8486912]{0:T(1024)(128)(4,1)}), s8[4194304]{0:T(1024)(128)(4,1)S(1)}, s32[]{:S(2)}) async-start(s8[8486912]{0:T(1024)(128)(4,1)} %bitcast.29), calls=%async_computation.2 | async-start | bytes 8388608
  66.9 15.4 %slice-start.1 = ((s8[8486912]{0:T(1024)(128)(4,1)}), s8[4194304]{0:T(1024)(128)(4,1)S(1)}, s32[]{:S(2)}) async-start(s8[8486912]{0:T(1024)(128)(4,1)} %bitcast.29), calls=%async_computation.3 | async-start | bytes 8388608
  74.4 7.8 slice-start.2
  87.4 3.1 copy-start.5
  87.4 11.9 %collective-permute-start.2 = (f32[1024,1792]{1,0:T(8,128)S(1)}, f32[1024,1792]{1,0:T(8,128)}, u32[]{:S(2)}, u32[]{:S(2)}) collective-permute-start(f32[1024,1792]{1,0:T(8,128)S(1)} %convolution_multiply_fusion.2), channel_id=1, source_target_pairs={{0,1},{1,0},{2,3},{3,2},{4,5},{5,4},{6,7},{7,6},{8,9},{9,8},{10,11... | collective-permute-start | bytes 22020104 | tf_op jit(solution)/shard_map/ppermute | solution.py:16
  105.4 160.3 %collective-permute-start.3 = (f32[1024,1792]{1,0:T(8,128)S(1)}, f32[1024,1792]{1,0:T(8,128)}, u32[]{:S(2)}, u32[]{:S(2)}) collective-permute-start(f32[1024,1792]{1,0:T(8,128)S(1)} %add.56), channel_id=1, source_target_pairs={{0,2},{1,3},{2,0},{3,1},{4,6},{5,7},{6,4},{7,5},{8,10},{9,11},{10,... | collective-permute-start | bytes 22020104 | tf_op jit(solution)/shard_map/ppermute | solution.py:16
  106.9 167.9 %copy-start.7 = (f32[4]{0:T(128)S(1)}, f32[4]{0:T(128)}, u32[]{:S(2)}) copy-start(f32[4]{0:T(128)} %param.17) | copy-start | bytes 52
  106.9 223.6 %collective-permute-start.1 = (f32[1184,1792]{1,0:T(8,128)}, f32[1184,1792]{1,0:T(8,128)}, u32[]{:S(2)}, u32[]{:S(2)}) collective-permute-start(f32[1184,1792]{1,0:T(8,128)} %bitcast.27), channel_id=1, source_target_pairs={{0,8},{8,16},{16,24},{24,0},{1,9},{9,17},{17,25},{25,1},{2,10},{10... | collective-permute-start | bytes 25460744 | tf_op jit(solution)/shard_map/ppermute | solution.py:30
  108.4 366.3 %collective-permute-start = (f32[1184,1792]{1,0:T(8,128)}, f32[1184,1792]{1,0:T(8,128)}, u32[]{:S(2)}, u32[]{:S(2)}) collective-permute-start(f32[1184,1792]{1,0:T(8,128)} %bitcast.28), channel_id=1, source_target_pairs={{0,24},{8,0},{16,8},{24,16},{1,25},{9,1},{17,9},{25,17},{2,26},{10... | collective-permute-start | bytes 25460744 | tf_op jit(solution)/shard_map/ppermute | solution.py:30
  272.5 202.2 %collective-permute-start.4 = (f32[1024,1792]{1,0:T(8,128)}, f32[1024,1792]{1,0:T(8,128)}, u32[]{:S(2)}, u32[]{:S(2)}) collective-permute-start(f32[1024,1792]{1,0:T(8,128)} %add.57), channel_id=1, source_target_pairs={{0,4},{1,5},{2,6},{3,7},{4,0},{5,1},{6,2},{7,3},{8,12},{9,13},{10,... | collective-permute-start | bytes 22020104 | tf_op jit(solution)/shard_map/ppermute | solution.py:16
  510.2 2.9 copy-start.6
  510.2 11.9 %collective-permute-start.7 = (f32[1024,1792]{1,0:T(8,128)S(1)}, f32[1024,1792]{1,0:T(8,128)}, u32[]{:S(2)}, u32[]{:S(2)}) collective-permute-start(f32[1024,1792]{1,0:T(8,128)S(1)} %convolution_multiply_fusion.1), channel_id=1, source_target_pairs={{0,1},{1,0},{2,3},{3,2},{4,5},{5,4},{6,7},{7,6},{8,9},{9,8},{10,11... | collective-permute-start | bytes 22020104 | tf_op jit(solution)/shard_map/ppermute | solution.py:16
  528.1 4.5 copy-start.3
  528.1 160.2 %collective-permute-start.8 = (f32[1024,1792]{1,0:T(8,128)S(1)}, f32[1024,1792]{1,0:T(8,128)}, u32[]{:S(2)}, u32[]{:S(2)}) collective-permute-start(f32[1024,1792]{1,0:T(8,128)S(1)} %add.61), channel_id=1, source_target_pairs={{0,2},{1,3},{2,0},{3,1},{4,6},{5,7},{6,4},{7,5},{8,10},{9,11},{10,... | collective-permute-start | bytes 22020104 | tf_op jit(solution)/shard_map/ppermute | solution.py:16
  528.8 187.6 %collective-permute-start.6 = (f32[1184,1792]{1,0:T(8,128)}, f32[1184,1792]{1,0:T(8,128)}, u32[]{:S(2)}, u32[]{:S(2)}) collective-permute-start(f32[1184,1792]{1,0:T(8,128)} %get-tuple-element.8), channel_id=1, source_target_pairs={{0,8},{8,16},{16,24},{24,0},{1,9},{9,17},{17,25},{25,1},{2,10},{10... | collective-permute-start | bytes 25460744 | tf_op jit(solution)/shard_map/ppermute | solution.py:30
  529.9 366.2 %collective-permute-start.5 = (f32[1184,1792]{1,0:T(8,128)}, f32[1184,1792]{1,0:T(8,128)}, u32[]{:S(2)}, u32[]{:S(2)}) collective-permute-start(f32[1184,1792]{1,0:T(8,128)} %get-tuple-element.8), channel_id=1, source_target_pairs={{0,24},{8,0},{16,8},{24,16},{1,25},{9,1},{17,9},{25,17},{2,26},{10... | collective-permute-start | bytes 25460744 | tf_op jit(solution)/shard_map/ppermute | solution.py:30
  694.4 2.9 copy-start.2
  697.2 198.9 %collective-permute-start.9 = (f32[1024,1792]{1,0:T(8,128)S(1)}, f32[1024,1792]{1,0:T(8,128)S(1)}, u32[]{:S(2)}, u32[]{:S(2)}) collective-permute-start(f32[1024,1792]{1,0:T(8,128)S(1)} %add.62), channel_id=1, source_target_pairs={{0,4},{1,5},{2,6},{3,7},{4,0},{5,1},{6,2},{7,3},{8,12},{9,13},{10,... | collective-permute-start | bytes 22020104 | tf_op jit(solution)/shard_map/ppermute | solution.py:16
  896.1 3.0 copy-start.4
  899.2 23.7 %copy-start.1 = (s32[4,1024]{1,0:T(4,128)S(1)}, s32[4,1024]{1,0:T(4,128)}, u32[]{:S(2)}) copy-start(s32[4,1024]{1,0:T(4,128)} %param.15) | copy-start | bytes 49156
Sparse Core Ops, SparseCore 0:
  29.7 37.0 all-gather.2
  274.9 49.4 all-gather.4
